TPU v7x, 32 devices: a whole 2x2x4 slice. The times are simulated.
32 devices in a mesh: gx: 4 (over z), gy: 4 (over y, core), gz: 2 (over x).
Axes of the slice: x: 2, y: 2, z: 4, core: 2. Of those that a mesh axis runs over, the one named last changes fastest.
Arguments:
- positions_now: float32 [32, 16, 2, 4, 128], P('gx', 'gy', 'gz'), may hold values from 0 to 1
- velocities: float32 [32, 16, 2, 3, 128], P('gx', 'gy', 'gz'), may hold values from -6 to 6
- positions_next: float32 [32, 16, 2, 3, 128], P('gx', 'gy', 'gz'), may hold values from 0 to 1
- halo_counts: int32 [32, 16, 2], P('gx', 'gy', 'gz'), may hold values from 1 to 128, as said below
- neighbour_lists: int32 [32, 16, 2, 14], P('gx', 'gy', 'gz'), may hold values from 0 to 26, as said below
- descendants: int32 [32, 16, 2, 2, 128], P('gx', 'gy', 'gz'), may hold values from 0 to 127, as said below
Outputs:
- drift: float32 [32, 16, 2, 3, 128], P('gx', 'gy', 'gz')
- tension: float32 [32, 16, 2, 128], P('gx', 'gy', 'gz')
Inputs may be any that keep to these rules, and one draw needn't show every extreme that they name: `halo_counts`: every cell holds 1 to 128 live halos; some cell holds exactly 128. `neighbour_lists`: each cell's list begins with code 13 (the cell itself) and holds distinct codes. `descendants`: row 0 is a code 0 to 26; row 1 is a live slot of the descendant's cell.
All inputs are finite; a program needn't handle non-finite values.
Results may differ from a plain program's by a relative error of at most 0.0003.
Values sent between devices are 32-bit elements; how exact they have to be, the bound alone decides.
A program may use at most 64 MiB of HBM per device.

v0:
```python
import jax
import jax.numpy as jnp
from jax import lax
from jax.sharding import PartitionSpec as P

EPS_SQ = 0.01
STEP_DT = 0.3
HALF_KICK = 0.045


def shifted(shard, axis, by):
    peers = lax.axis_size(axis)
    return lax.ppermute(shard, axis, [(i, (i + by) % peers) for i in range(peers)])


def offsets_of(code):
    return (code // 9 - 1, code // 3 % 3 - 1, code % 3 - 1)


def stack_state(positions_now, positions_next, halo_counts):
    slots = positions_now.shape[-1]
    live = (
        jnp.arange(slots, dtype=jnp.int32)[None, None, None, :] < halo_counts[..., None]
    ).astype(jnp.float32)
    masses = positions_now[:, :, :, 3:4, :] * live[:, :, :, None, :]
    return (jnp.concatenate([positions_now[:, :, :, :3, :], masses, positions_next], axis=3), live)


def predict(padded, neighbour_lists, velocities, descendants, halo_counts):
    cx, cy, cz = neighbour_lists.shape[:3]
    width = neighbour_lists.shape[3]
    px, py, pz = (cx + 2, cy + 2, cz + 2)
    slots = padded.shape[-1]
    cells = cx * cy * cz
    flat = padded.reshape(px * py * pz, 7, slots)
    next_rows = jnp.transpose(flat[:, 4:7, :], (0, 2, 1)).reshape(px * py * pz * slots, 3)
    grid = jnp.indices((cx, cy, cz), dtype=jnp.int32).reshape(3, cells)
    base = ((grid[0] + 1) * py + grid[1] + 1) * pz + grid[2] + 1
    group = 32
    blocks = cells // group
    lists = neighbour_lists.reshape(blocks, group, width)
    vel = velocities.reshape(blocks, group, 3, slots)
    desc = descendants.reshape(blocks, group, 2, slots)
    counts = halo_counts.reshape(blocks, group)
    bases = base.reshape(blocks, group)

    def one_group(items):
        base_g, list_g, vel_g, desc_g, count_g = items
        own = flat[base_g]
        pos = own[:, :3, :]

        def step(accel, code):
            dx, dy, dz = offsets_of(code)
            source = flat[base_g + dx * py * pz + dy * pz + dz]
            offset = jnp.stack([dx, dy, dz], 1).astype(jnp.float32)
            spot = offset[:, :, None] + source[:, :3, :]
            diff = spot[:, :, None, :] - pos[:, :, :, None]
            dist_sq = jnp.sum(diff * diff, axis=1) + EPS_SQ
            weight = source[:, 3, None, :] / (dist_sq * jnp.sqrt(dist_sq))
            return (accel + jnp.sum(diff * weight[:, None, :, :], axis=3), None)

        accel, _ = lax.scan(step, jnp.zeros(pos.shape, jnp.float32), jnp.transpose(list_g))
        predicted = pos + STEP_DT * vel_g + HALF_KICK * accel
        dcode = desc_g[:, 0, :]
        dslot = desc_g[:, 1, :]
        ddx, ddy, ddz = offsets_of(dcode)
        target = base_g[:, None] + ddx * py * pz + ddy * pz + ddz
        found = jnp.transpose(next_rows[target * slots + dslot], (0, 2, 1))
        offset = jnp.stack([ddx, ddy, ddz], 1).astype(jnp.float32)
        error = offset + found - predicted
        live = (jnp.arange(slots, dtype=jnp.int32)[None, :] < count_g[:, None]).astype(jnp.float32)
        drift = error * live[:, None, :]
        squared = jnp.sum(error * error, axis=1) * live
        return (drift, squared)

    drift, squared = lax.map(one_group, (bases, lists, vel, desc, counts))
    return (drift.reshape(cx, cy, cz, 3, slots), squared.reshape(cx, cy, cz, slots))


def shards(positions_now, velocities, positions_next, halo_counts, neighbour_lists, descendants):
    state, live = stack_state(positions_now, positions_next, halo_counts)
    below = shifted(state[-1:], "gx", 1)
    above = shifted(state[:1], "gx", -1)
    state = jnp.concatenate([below, state, above], axis=0)
    below = shifted(state[:, -1:], "gy", 1)
    above = shifted(state[:, :1], "gy", -1)
    state = jnp.concatenate([below, state, above], axis=1)
    below = shifted(state, "gz", 1)
    above = shifted(state, "gz", -1)
    padded = jnp.concatenate([below, state, above], axis=2)
    drift, squared = predict(padded, neighbour_lists, velocities, descendants, halo_counts)
    total_sq, total_live = lax.psum((jnp.sum(squared), jnp.sum(live)), ("gx", "gy", "gz"))
    mean_sq = total_sq / total_live
    return (drift, squared / (mean_sq + 1e-06))


def solution(mesh):
    return jax.shard_map(
        shards,
        mesh=mesh,
        in_specs=(
            P("gx", "gy", "gz", None, None),
            P("gx", "gy", "gz", None, None),
            P("gx", "gy", "gz", None, None),
            P("gx", "gy", "gz"),
            P("gx", "gy", "gz", None),
            P("gx", "gy", "gz", None, None),
        ),
        out_specs=(P("gx", "gy", "gz", None, None), P("gx", "gy", "gz", None)),
        check_vma=False,
    )
```

profile of v0, /device:TPU:0, one launch (start us, length us, event | category | flops | bytes accessed | tf_op | source)
XLA Modules:
  0.0 198.5 jit_solution(14969671886420525400)
XLA Ops:
  0.6 0.8 copy.106
  1.4 0.8 slice.74
  2.2 0.8 compare_select_fusion.1
  3.0 0.7 pad_maximum_fusion.9
  3.8 5.1 %collective-permute-start.1 = (f32[1,4,1,7,128]{4,2,3,1,0:T(1,128)S(1)}, f32[1,4,1,7,128]{4,2,3,1,0:T(1,128)S(1)}, u32[]{:S(2)}, u32[]{:S(2)}) collective-permute-start(f32[1,4,1,7,128]{4,2,3,1,0:T(1,128)S(1)} %get-tuple-element.218), channel_id=1, source_target_pairs={{0,24},{8,0},{16,8},{24,16},{1,25},{9,1},{17,9},{25,17},{2,26},{10... | collective-permute-start | bytes 43016 | tf_op jit(solution)/shard_map/ppermute | solution.py:13
  9.2 0.9 broadcast_multiply_fusion.1
  10.0 0.8 copy.104
  11.0 0.8 fusion.30
  11.7 2.7 %collective-permute-done = f32[1,4,1,7,128]{4,2,3,1,0:T(1,128)S(1)} collective-permute-done((f32[1,4,1,7,128]{4,2,3,1,0:T(1,128)S(1)}, f32[1,4,1,7,128]{4,2,3,1,0:T(1,128)S(1)}, u32[]{:S(2)}, u32[]{:S(2)}) %collective-permute-start) | collective-permute-done | bytes 14368 | tf_op jit(solution)/shard_map/ppermute | solution.py:13
  14.4 0.8 pad_maximum_fusion.6
  15.8 0.8 copy.116
  16.5 0.8 copy.113
  17.4 1.6 collective-permute-done.2
  19.1 1.0 pad_maximum_fusion.1
  20.1 1.6 collective-permute-start.4
  21.7 5.8 %collective-permute-done.4 = f32[10,6,1,7,128]{4,2,3,1,0:T(1,128)S(1)} collective-permute-done((f32[10,6,1,7,128]{4,2,3,1,0:T(1,128)S(1)}, f32[10,6,1,7,128]{4,2,3,1,0:T(1,128)S(1)}, u32[]{:S(2)}, u32[]{:S(2)}) %collective-permute-start.4) | collective-permute-done | bytes 215072 | tf_op jit(solution)/shard_map/ppermute | solution.py:13
  27.5 1.3 pad_maximum_fusion
  29.6 106.7 %while.22 = (s32[]{:T(128)}, f32[32,3,128]{2,1,0:T(4,128)S(1)}, s32[14,32]{1,0:T(8,128)S(1)}, f32[180,7,128]{2,1,0:T(8,128)S(1)}, f32[32,3,128]{2,1,0:T(4,128)S(1)}, /*index=5*/s32[]{:T(128)}, s32[]{:T(128)}) while((s32[]{:T(128)}, f32[32,3,128]{2,1,0:T(4,128)S(1)}, s32[14,32]{1,0:T(8,128)S(1)}, f32[180,7,128]{2,1,0:T(8,128)S(1)}, ...), condition=%wide.region_3.4_spmd.clone, body=%wide.region_0.3_spmd.clone.sunk | while | flops 10512963 | bytes 9166179 | solution.py:62
  30.6 2.1 %fusion.45 = f32[32,128,128]{2,1,0:T(8,128)S(1)} fusion(f32[32,3,128]{2,1,0:T(4,128)S(1)} %get-tuple-element.279, f32[32,3,128]{2,1,0:T(4,128)S(1)} %slice_add_fusion.2), kind=kLoop, calls=%fused_computation.6.clone.1 | loop fusion | flops 4194304 | bytes 2195456 | tf_op jit(solution)/shard_map/while/body/eval_jaxpr/while/body/eval_jaxpr/reduce_sum | solution.py:58
  32.7 0.8 fusion.46
  33.4 3.7 %fusion.47 = f32[32,3,128]{2,1,0:T(4,128)S(1)} fusion(f32[32,128,128]{2,1,0:T(8,128)S(1)} %fusion.46, f32[32,3,128]{2,1,0:T(4,128)S(1)} %get-tuple-element.279, f32[32,3,128]{2,1,0:T(4,128)S(1)} %slice_add_fusion.2), kind=kLoop, calls=%fused_computation.7.clone.1 | loop fusion | flops 4706304 | bytes 2244608 | tf_op jit(solution)/shard_map/while/body/eval_jaxpr/while/body/eval_jaxpr/reduce_sum | solution.py:60
  38.2 2.1 %fusion.45 = f32[32,128,128]{2,1,0:T(8,128)S(1)} fusion(f32[32,3,128]{2,1,0:T(4,128)S(1)} %get-tuple-element.279, f32[32,3,128]{2,1,0:T(4,128)S(1)} %slice_add_fusion.2), kind=kLoop, calls=%fused_computation.6.clone.1 | loop fusion | flops 4194304 | bytes 2195456 | tf_op jit(solution)/shard_map/while/body/eval_jaxpr/while/body/eval_jaxpr/reduce_sum | solution.py:58
  40.3 0.8 fusion.46
  41.0 3.7 %fusion.47 = f32[32,3,128]{2,1,0:T(4,128)S(1)} fusion(f32[32,128,128]{2,1,0:T(8,128)S(1)} %fusion.46, f32[32,3,128]{2,1,0:T(4,128)S(1)} %get-tuple-element.279, f32[32,3,128]{2,1,0:T(4,128)S(1)} %slice_add_fusion.2), kind=kLoop, calls=%fused_computation.7.clone.1 | loop fusion | flops 4706304 | bytes 2244608 | tf_op jit(solution)/shard_map/while/body/eval_jaxpr/while/body/eval_jaxpr/reduce_sum | solution.py:60
  45.8 2.1 %fusion.45 = f32[32,128,128]{2,1,0:T(8,128)S(1)} fusion(f32[32,3,128]{2,1,0:T(4,128)S(1)} %get-tuple-element.279, f32[32,3,128]{2,1,0:T(4,128)S(1)} %slice_add_fusion.2), kind=kLoop, calls=%fused_computation.6.clone.1 | loop fusion | flops 4194304 | bytes 2195456 | tf_op jit(solution)/shard_map/while/body/eval_jaxpr/while/body/eval_jaxpr/reduce_sum | solution.py:58
  47.9 0.8 fusion.46
  48.7 3.7 %fusion.47 = f32[32,3,128]{2,1,0:T(4,128)S(1)} fusion(f32[32,128,128]{2,1,0:T(8,128)S(1)} %fusion.46, f32[32,3,128]{2,1,0:T(4,128)S(1)} %get-tuple-element.279, f32[32,3,128]{2,1,0:T(4,128)S(1)} %slice_add_fusion.2), kind=kLoop, calls=%fused_computation.7.clone.1 | loop fusion | flops 4706304 | bytes 2244608 | tf_op jit(solution)/shard_map/while/body/eval_jaxpr/while/body/eval_jaxpr/reduce_sum | solution.py:60
  53.4 2.1 %fusion.45 = f32[32,128,128]{2,1,0:T(8,128)S(1)} fusion(f32[32,3,128]{2,1,0:T(4,128)S(1)} %get-tuple-element.279, f32[32,3,128]{2,1,0:T(4,128)S(1)} %slice_add_fusion.2), kind=kLoop, calls=%fused_computation.6.clone.1 | loop fusion | flops 4194304 | bytes 2195456 | tf_op jit(solution)/shard_map/while/body/eval_jaxpr/while/body/eval_jaxpr/reduce_sum | solution.py:58
  55.5 0.8 fusion.46
  56.3 3.7 %fusion.47 = f32[32,3,128]{2,1,0:T(4,128)S(1)} fusion(f32[32,128,128]{2,1,0:T(8,128)S(1)} %fusion.46, f32[32,3,128]{2,1,0:T(4,128)S(1)} %get-tuple-element.279, f32[32,3,128]{2,1,0:T(4,128)S(1)} %slice_add_fusion.2), kind=kLoop, calls=%fused_computation.7.clone.1 | loop fusion | flops 4706304 | bytes 2244608 | tf_op jit(solution)/shard_map/while/body/eval_jaxpr/while/body/eval_jaxpr/reduce_sum | solution.py:60
  61.0 2.1 %fusion.45 = f32[32,128,128]{2,1,0:T(8,128)S(1)} fusion(f32[32,3,128]{2,1,0:T(4,128)S(1)} %get-tuple-element.279, f32[32,3,128]{2,1,0:T(4,128)S(1)} %slice_add_fusion.2), kind=kLoop, calls=%fused_computation.6.clone.1 | loop fusion | flops 4194304 | bytes 2195456 | tf_op jit(solution)/shard_map/while/body/eval_jaxpr/while/body/eval_jaxpr/reduce_sum | solution.py:58
  63.1 0.8 fusion.46
  63.9 3.7 %fusion.47 = f32[32,3,128]{2,1,0:T(4,128)S(1)} fusion(f32[32,128,128]{2,1,0:T(8,128)S(1)} %fusion.46, f32[32,3,128]{2,1,0:T(4,128)S(1)} %get-tuple-element.279, f32[32,3,128]{2,1,0:T(4,128)S(1)} %slice_add_fusion.2), kind=kLoop, calls=%fused_computation.7.clone.1 | loop fusion | flops 4706304 | bytes 2244608 | tf_op jit(solution)/shard_map/while/body/eval_jaxpr/while/body/eval_jaxpr/reduce_sum | solution.py:60
  68.7 2.1 %fusion.45 = f32[32,128,128]{2,1,0:T(8,128)S(1)} fusion(f32[32,3,128]{2,1,0:T(4,128)S(1)} %get-tuple-element.279, f32[32,3,128]{2,1,0:T(4,128)S(1)} %slice_add_fusion.2), kind=kLoop, calls=%fused_computation.6.clone.1 | loop fusion | flops 4194304 | bytes 2195456 | tf_op jit(solution)/shard_map/while/body/eval_jaxpr/while/body/eval_jaxpr/reduce_sum | solution.py:58
  70.8 0.8 fusion.46
  71.5 3.7 %fusion.47 = f32[32,3,128]{2,1,0:T(4,128)S(1)} fusion(f32[32,128,128]{2,1,0:T(8,128)S(1)} %fusion.46, f32[32,3,128]{2,1,0:T(4,128)S(1)} %get-tuple-element.279, f32[32,3,128]{2,1,0:T(4,128)S(1)} %slice_add_fusion.2), kind=kLoop, calls=%fused_computation.7.clone.1 | loop fusion | flops 4706304 | bytes 2244608 | tf_op jit(solution)/shard_map/while/body/eval_jaxpr/while/body/eval_jaxpr/reduce_sum | solution.py:60
  76.3 2.1 %fusion.45 = f32[32,128,128]{2,1,0:T(8,128)S(1)} fusion(f32[32,3,128]{2,1,0:T(4,128)S(1)} %get-tuple-element.279, f32[32,3,128]{2,1,0:T(4,128)S(1)} %slice_add_fusion.2), kind=kLoop, calls=%fused_computation.6.clone.1 | loop fusion | flops 4194304 | bytes 2195456 | tf_op jit(solution)/shard_map/while/body/eval_jaxpr/while/body/eval_jaxpr/reduce_sum | solution.py:58
  78.4 0.8 fusion.46
  79.2 3.7 %fusion.47 = f32[32,3,128]{2,1,0:T(4,128)S(1)} fusion(f32[32,128,128]{2,1,0:T(8,128)S(1)} %fusion.46, f32[32,3,128]{2,1,0:T(4,128)S(1)} %get-tuple-element.279, f32[32,3,128]{2,1,0:T(4,128)S(1)} %slice_add_fusion.2), kind=kLoop, calls=%fused_computation.7.clone.1 | loop fusion | flops 4706304 | bytes 2244608 | tf_op jit(solution)/shard_map/while/body/eval_jaxpr/while/body/eval_jaxpr/reduce_sum | solution.py:60
  83.9 2.1 %fusion.45 = f32[32,128,128]{2,1,0:T(8,128)S(1)} fusion(f32[32,3,128]{2,1,0:T(4,128)S(1)} %get-tuple-element.279, f32[32,3,128]{2,1,0:T(4,128)S(1)} %slice_add_fusion.2), kind=kLoop, calls=%fused_computation.6.clone.1 | loop fusion | flops 4194304 | bytes 2195456 | tf_op jit(solution)/shard_map/while/body/eval_jaxpr/while/body/eval_jaxpr/reduce_sum | solution.py:58
  86.0 0.8 fusion.46
  86.8 3.7 %fusion.47 = f32[32,3,128]{2,1,0:T(4,128)S(1)} fusion(f32[32,128,128]{2,1,0:T(8,128)S(1)} %fusion.46, f32[32,3,128]{2,1,0:T(4,128)S(1)} %get-tuple-element.279, f32[32,3,128]{2,1,0:T(4,128)S(1)} %slice_add_fusion.2), kind=kLoop, calls=%fused_computation.7.clone.1 | loop fusion | flops 4706304 | bytes 2244608 | tf_op jit(solution)/shard_map/while/body/eval_jaxpr/while/body/eval_jaxpr/reduce_sum | solution.py:60
  91.5 2.1 %fusion.45 = f32[32,128,128]{2,1,0:T(8,128)S(1)} fusion(f32[32,3,128]{2,1,0:T(4,128)S(1)} %get-tuple-element.279, f32[32,3,128]{2,1,0:T(4,128)S(1)} %slice_add_fusion.2), kind=kLoop, calls=%fused_computation.6.clone.1 | loop fusion | flops 4194304 | bytes 2195456 | tf_op jit(solution)/shard_map/while/body/eval_jaxpr/while/body/eval_jaxpr/reduce_sum | solution.py:58
  93.6 0.8 fusion.46
  94.4 3.7 %fusion.47 = f32[32,3,128]{2,1,0:T(4,128)S(1)} fusion(f32[32,128,128]{2,1,0:T(8,128)S(1)} %fusion.46, f32[32,3,128]{2,1,0:T(4,128)S(1)} %get-tuple-element.279, f32[32,3,128]{2,1,0:T(4,128)S(1)} %slice_add_fusion.2), kind=kLoop, calls=%fused_computation.7.clone.1 | loop fusion | flops 4706304 | bytes 2244608 | tf_op jit(solution)/shard_map/while/body/eval_jaxpr/while/body/eval_jaxpr/reduce_sum | solution.py:60
  99.1 2.1 %fusion.45 = f32[32,128,128]{2,1,0:T(8,128)S(1)} fusion(f32[32,3,128]{2,1,0:T(4,128)S(1)} %get-tuple-element.279, f32[32,3,128]{2,1,0:T(4,128)S(1)} %slice_add_fusion.2), kind=kLoop, calls=%fused_computation.6.clone.1 | loop fusion | flops 4194304 | bytes 2195456 | tf_op jit(solution)/shard_map/while/body/eval_jaxpr/while/body/eval_jaxpr/reduce_sum | solution.py:58
  101.3 0.8 fusion.46
  102.0 3.7 %fusion.47 = f32[32,3,128]{2,1,0:T(4,128)S(1)} fusion(f32[32,128,128]{2,1,0:T(8,128)S(1)} %fusion.46, f32[32,3,128]{2,1,0:T(4,128)S(1)} %get-tuple-element.279, f32[32,3,128]{2,1,0:T(4,128)S(1)} %slice_add_fusion.2), kind=kLoop, calls=%fused_computation.7.clone.1 | loop fusion | flops 4706304 | bytes 2244608 | tf_op jit(solution)/shard_map/while/body/eval_jaxpr/while/body/eval_jaxpr/reduce_sum | solution.py:60
  106.8 2.1 %fusion.45 = f32[32,128,128]{2,1,0:T(8,128)S(1)} fusion(f32[32,3,128]{2,1,0:T(4,128)S(1)} %get-tuple-element.279, f32[32,3,128]{2,1,0:T(4,128)S(1)} %slice_add_fusion.2), kind=kLoop, calls=%fused_computation.6.clone.1 | loop fusion | flops 4194304 | bytes 2195456 | tf_op jit(solution)/shard_map/while/body/eval_jaxpr/while/body/eval_jaxpr/reduce_sum | solution.py:58
  108.9 0.8 fusion.46
  109.6 3.7 %fusion.47 = f32[32,3,128]{2,1,0:T(4,128)S(1)} fusion(f32[32,128,128]{2,1,0:T(8,128)S(1)} %fusion.46, f32[32,3,128]{2,1,0:T(4,128)S(1)} %get-tuple-element.279, f32[32,3,128]{2,1,0:T(4,128)S(1)} %slice_add_fusion.2), kind=kLoop, calls=%fused_computation.7.clone.1 | loop fusion | flops 4706304 | bytes 2244608 | tf_op jit(solution)/shard_map/while/body/eval_jaxpr/while/body/eval_jaxpr/reduce_sum | solution.py:60
  114.4 2.1 %fusion.45 = f32[32,128,128]{2,1,0:T(8,128)S(1)} fusion(f32[32,3,128]{2,1,0:T(4,128)S(1)} %get-tuple-element.279, f32[32,3,128]{2,1,0:T(4,128)S(1)} %slice_add_fusion.2), kind=kLoop, calls=%fused_computation.6.clone.1 | loop fusion | flops 4194304 | bytes 2195456 | tf_op jit(solution)/shard_map/while/body/eval_jaxpr/while/body/eval_jaxpr/reduce_sum | solution.py:58
  116.5 0.8 fusion.46
  117.3 3.7 %fusion.47 = f32[32,3,128]{2,1,0:T(4,128)S(1)} fusion(f32[32,128,128]{2,1,0:T(8,128)S(1)} %fusion.46, f32[32,3,128]{2,1,0:T(4,128)S(1)} %get-tuple-element.279, f32[32,3,128]{2,1,0:T(4,128)S(1)} %slice_add_fusion.2), kind=kLoop, calls=%fused_computation.7.clone.1 | loop fusion | flops 4706304 | bytes 2244608 | tf_op jit(solution)/shard_map/while/body/eval_jaxpr/while/body/eval_jaxpr/reduce_sum | solution.py:60
  122.0 2.1 %fusion.45 = f32[32,128,128]{2,1,0:T(8,128)S(1)} fusion(f32[32,3,128]{2,1,0:T(4,128)S(1)} %get-tuple-element.279, f32[32,3,128]{2,1,0:T(4,128)S(1)} %slice_add_fusion.2), kind=kLoop, calls=%fused_computation.6.clone.1 | loop fusion | flops 4194304 | bytes 2195456 | tf_op jit(solution)/shard_map/while/body/eval_jaxpr/while/body/eval_jaxpr/reduce_sum | solution.py:58
  124.1 0.8 fusion.46
  124.9 3.7 %fusion.47 = f32[32,3,128]{2,1,0:T(4,128)S(1)} fusion(f32[32,128,128]{2,1,0:T(8,128)S(1)} %fusion.46, f32[32,3,128]{2,1,0:T(4,128)S(1)} %get-tuple-element.279, f32[32,3,128]{2,1,0:T(4,128)S(1)} %slice_add_fusion.2), kind=kLoop, calls=%fused_computation.7.clone.1 | loop fusion | flops 4706304 | bytes 2244608 | tf_op jit(solution)/shard_map/while/body/eval_jaxpr/while/body/eval_jaxpr/reduce_sum | solution.py:60
  129.6 2.1 %fusion.45 = f32[32,128,128]{2,1,0:T(8,128)S(1)} fusion(f32[32,3,128]{2,1,0:T(4,128)S(1)} %get-tuple-element.279, f32[32,3,128]{2,1,0:T(4,128)S(1)} %slice_add_fusion.2), kind=kLoop, calls=%fused_computation.6.clone.1 | loop fusion | flops 4194304 | bytes 2195456 | tf_op jit(solution)/shard_map/while/body/eval_jaxpr/while/body/eval_jaxpr/reduce_sum | solution.py:58
  131.7 0.8 fusion.46
  132.5 3.7 %fusion.47 = f32[32,3,128]{2,1,0:T(4,128)S(1)} fusion(f32[32,128,128]{2,1,0:T(8,128)S(1)} %fusion.46, f32[32,3,128]{2,1,0:T(4,128)S(1)} %get-tuple-element.279, f32[32,3,128]{2,1,0:T(4,128)S(1)} %slice_add_fusion.2), kind=kLoop, calls=%fused_computation.7.clone.1 | loop fusion | flops 4706304 | bytes 2244608 | tf_op jit(solution)/shard_map/while/body/eval_jaxpr/while/body/eval_jaxpr/reduce_sum | solution.py:60
  136.3 5.9 %copy.109 = f32[180,128,3]{2,1,0:T(8,128)} copy(f32[180,128,3]{1,2,0:T(4,128)S(1)} %slice_bitcast_fusion) | data formatting | bytes 552960 | tf_op jit(solution)/shard_map/transpose | solution.py:36
  142.3 15.1 %gather_fusion.1 = f32[4096,3]{1,0:T(8,128)S(1)} fusion(f32[23040,3]{1,0:T(8,128)} %bitcast.118, s32[4096]{0:T(1024)S(1)} %get-tuple-element.212), kind=kCustom, calls=%fused_computation.1 | custom fusion | bytes 114688 | tf_op jit(solution)/shard_map/while/body/eval_jaxpr/gather | solution.py:68
  159.4 37.1 %all-reduce = (f32[]{:T(128)}, f32[]{:T(128)}) all-reduce(f32[]{:T(128)} %select_reduce_fusion, f32[]{:T(128)} %fusion.30), channel_id=1, replica_groups=mesh['gx'=4,'gy'=4,'gz'=2] {'gx','gy','gz'}, use_global_device_ids=true, to_apply=%region_6.7 | all-reduce | flops 2 | bytes 16 | tf_op jit(solution)/shard_map/psum | solution.py:92
  197.8 0.7 fusion.29
  (167 shorter events, 18.0 us)
Async XLA Ops:
  3.8 7.9 %collective-permute-start.1 = (f32[1,4,1,7,128]{4,2,3,1,0:T(1,128)S(1)}, f32[1,4,1,7,128]{4,2,3,1,0:T(1,128)S(1)}, u32[]{:S(2)}, u32[]{:S(2)}) collective-permute-start(f32[1,4,1,7,128]{4,2,3,1,0:T(1,128)S(1)} %get-tuple-element.218), channel_id=1, source_target_pairs={{0,24},{8,0},{16,8},{24,16},{1,25},{9,1},{17,9},{25,17},{2,26},{10... | collective-permute-start | bytes 43016 | tf_op jit(solution)/shard_map/ppermute | solution.py:13
  8.9 5.5 %collective-permute-start = (f32[1,4,1,7,128]{4,2,3,1,0:T(1,128)S(1)}, f32[1,4,1,7,128]{4,2,3,1,0:T(1,128)S(1)}, u32[]{:S(2)}, u32[]{:S(2)}) collective-permute-start(f32[1,4,1,7,128]{4,2,3,1,0:T(1,128)S(1)} %get-tuple-element.217), channel_id=1, source_target_pairs={{0,8},{8,16},{16,24},{24,0},{1,9},{9,17},{17,25},{25,1},{2,10},{10... | collective-permute-start | bytes 43016 | tf_op jit(solution)/shard_map/ppermute | solution.py:13
  15.2 2.2 %collective-permute-start.3 = (f32[10,1,1,7,128]{4,2,3,1,0:T(1,128)S(1)}, f32[10,1,1,7,128]{4,2,3,1,0:T(1,128)S(1)}, u32[]{:S(2)}, u32[]{:S(2)}) collective-permute-start(f32[10,1,1,7,128]{4,2,3,1,0:T(1,128)S(1)} %get-tuple-element.216), channel_id=1, source_target_pairs={{0,6},{2,0},{4,2},{6,4},{1,7},{3,1},{5,3},{7,5},{8,14},{10,8},{12,... | collective-permute-start | bytes 107528 | tf_op jit(solution)/shard_map/ppermute | solution.py:13
  15.3 3.8 %collective-permute-start.2 = (f32[10,1,1,7,128]{4,2,3,1,0:T(1,128)S(1)}, f32[10,1,1,7,128]{4,2,3,1,0:T(1,128)S(1)}, u32[]{:S(2)}, u32[]{:S(2)}) collective-permute-start(f32[10,1,1,7,128]{4,2,3,1,0:T(1,128)S(1)} %get-tuple-element.215), channel_id=1, source_target_pairs={{0,2},{2,4},{4,6},{6,0},{1,3},{3,5},{5,7},{7,1},{8,10},{10,12},{12... | collective-permute-start | bytes 107528 | tf_op jit(solution)/shard_map/ppermute | solution.py:13
  20.1 7.4 %collective-permute-start.4 = (f32[10,6,1,7,128]{4,2,3,1,0:T(1,128)S(1)}, f32[10,6,1,7,128]{4,2,3,1,0:T(1,128)S(1)}, u32[]{:S(2)}, u32[]{:S(2)}) collective-permute-start(f32[10,6,1,7,128]{4,2,3,1,0:T(1,128)S(1)} %pad_maximum_fusion.1), channel_id=1, source_target_pairs={{0,1},{1,0},{2,3},{3,2},{4,5},{5,4},{6,7},{7,6},{8,9},{9,8},{10,11... | collective-permute-start | bytes 645128 | tf_op jit(solution)/shard_map/ppermute | solution.py:13
where the time goes:
time: 200 us; the launch traced here: 198 us
  other arithmetic  103 us (52%)
  local copies, waits for them, and re-layouts  38.2 us (19%)
  blocking collectives  37.1 us (19%)
  waiting for transfers between devices  10.1 us (5%)
  starting transfers between devices  7.24 us (4%)
  between operations  2.06 us (1%)
    reduce_sum x14, other arithmetic, step(): return (accel + jnp.sum(diff * weight[:, None, :, :], axis=3), None)  52.1 us
    psum x1, blocking collectives, shards(): lax.psum((jnp.sum(squared), jnp.sum(live)), ('gx', 'gy', 'gz'))  37.1 us
    reduce_sum x14, other arithmetic, step(): dist_sq = jnp.sum(diff * diff, axis=1) + EPS_SQ  28.9 us
    gather x2, local copies, waits for them, and re-layouts, one_group(): found = jnp.transpose(next_rows[target * slots + dslot], (0, 2, 1))  15.7 us
    div x14, other arithmetic, step(): weight = source[:, 3, None, :] / (dist_sq * jnp.sqrt(dist_sq))  10.7 us
    ppermute x5, waiting for transfers between devices, shifted(): lax.ppermute(shard, axis, [(i, (i + by) % peers) for i in range(peers)])  10.1 us
    gather x14, local copies, waits for them, and re-layouts, step(): source = flat[base_g + dx * py * pz + dy * pz + dz]  8.19 us
    ppermute x5, starting transfers between devices, shifted(): lax.ppermute(shard, axis, [(i, (i + by) % peers) for i in range(peers)])  7.24 us
  transfers between devices with their start and end apart: 5, of which 3 were waited for; matrix products, arithmetic and copies ran while one was open for 2% of the time, Pallas kernels for 0%

commit v1 on v0

v1 whole, which is shorter than its diff:
```python
import functools

import jax
import jax.numpy as jnp
from jax import lax
from jax.experimental import pallas as pl
from jax.experimental.pallas import tpu as pltpu
from jax.sharding import PartitionSpec as P

EPS_SQ = 0.01
STEP_DT = 0.3
HALF_KICK = 0.045


def shifted(shard, axis, by):
    peers = lax.axis_size(axis)
    return lax.ppermute(shard, axis, [(i, (i + by) % peers) for i in range(peers)])


def pieces(tile):
    first = tile.astype(jnp.bfloat16).astype(jnp.float32)
    rest = tile - first
    second = rest.astype(jnp.bfloat16).astype(jnp.float32)
    return first, second, rest - second


def kernel(dims, width, lists, padded, vel, desc, drift_ref, sq_ref, feat, moment, placed):
    cx, cy, cz = dims
    py, pz = cy + 2, cz + 2
    cells = cx * cy * cz
    slots = padded.shape[-1]
    row = lax.broadcasted_iota(jnp.int32, (8, slots), 0)

    def place(n, _):
        ix, iy, iz = n // (py * pz), n // pz % py, n % pz
        fx = ix.astype(jnp.float32) - (cx + 2) / 2
        fy = iy.astype(jnp.float32) - (cy + 2) / 2
        fz = iz.astype(jnp.float32) - (cz + 2) / 2
        shift = jnp.where(row % 4 == 0, fx, jnp.where(row % 4 == 1, fy, jnp.where(row % 4 == 2, fz, 0.0)))
        tile = padded[n] + shift
        placed[n] = tile
        mass = tile[3:4]
        norm = tile[0:1] * tile[0:1] + tile[1:2] * tile[1:2] + tile[2:3] * tile[2:3]
        ext = jnp.where(row < 3, tile, jnp.where(row == 3, norm, jnp.where(row == 4, 1.0, 0.0)))
        a, b, c = pieces(ext)
        feat[n] = jnp.concatenate([a, a, a, b, b, c], axis=0).astype(jnp.bfloat16)
        mom = jnp.where(row < 3, tile * mass, jnp.where(row == 3, mass, 0.0))
        moment[n] = jnp.concatenate(list(pieces(mom)) + [jnp.zeros_like(mom)], axis=0).astype(jnp.bfloat16)
        return 0

    lax.fori_loop(0, padded.shape[0], place, 0)

    def target(n, _):
        ix, iy, iz = n // (cy * cz), n // cz % cy, n % cz
        corner = (ix * py + iy) * pz + iz
        base = corner + (py + 1) * pz + 1
        own = placed[base]
        norm = own[0:1] * own[0:1] + own[1:2] * own[1:2] + own[2:3] * own[2:3]
        ext = jnp.where(row < 3, -2.0 * own, jnp.where(row == 3, 1.0, jnp.where(row == 4, norm + EPS_SQ, 0.0)))
        a, b, c = pieces(ext)
        lhs = jnp.concatenate([a, b, c, a, b, a], axis=0).T.astype(jnp.bfloat16)

        def source(k):
            code = lists[n * width + k]
            d9 = (code * 57) >> 9
            d3 = (code * 43) >> 7
            return corner + d9 * (py * pz) + (d3 - 3 * d9) * pz + code - 3 * d3

        acc = jnp.zeros((slots, 32), jnp.float32)
        for k in range(0, width, 2):
            cells_k = [source(j) for j in range(k, min(k + 2, width))]
            f = jnp.concatenate([feat[s] for s in cells_k], axis=1)
            z = jnp.concatenate([moment[s] for s in cells_k], axis=1)
            dist_sq = jnp.dot(lhs, f, preferred_element_type=jnp.float32)
            inv = lax.rsqrt(dist_sq)
            weight = inv * inv * inv
            high = weight.astype(jnp.bfloat16)
            low = (weight - high.astype(jnp.float32)).astype(jnp.bfloat16)
            dn = (((1,), (1,)), ((), ()))
            acc += lax.dot_general(high, z, dn, preferred_element_type=jnp.float32)
            acc += lax.dot_general(low, z, dn, preferred_element_type=jnp.float32)
        acc = acc.T
        sums = acc[0:8] + acc[8:16] + acc[16:24]
        accel = sums[0:3] - own[0:3] * sums[3:4]
        predicted = own[0:3] + STEP_DT * vel[n] + HALF_KICK * accel
        links = desc[n]
        dcode = jnp.broadcast_to(links[0:1], (8, slots))
        dslot = jnp.broadcast_to(links[1:2], (8, slots))
        found = jnp.zeros((8, slots), jnp.float32)
        for code in range(27):
            at = corner + (code // 9) * py * pz + (code // 3 % 3) * pz + code % 3
            got = jnp.take_along_axis(placed[at], dslot, axis=1)
            found = jnp.where(dcode == code, got, found)
        error = found[4:7] - predicted
        live = own[7:8]
        drift_ref[n] = error * live
        sq_ref[pl.ds(n, 1), :] = jnp.sum(error * error, axis=0, keepdims=True) * live
        return 0

    lax.fori_loop(0, cells, target, 0)


def shards(positions_now, velocities, positions_next, halo_counts, neighbour_lists, descendants):
    slots = positions_now.shape[-1]
    cx, cy, cz, width = neighbour_lists.shape
    cells = cx * cy * cz
    live = (
        jnp.arange(slots, dtype=jnp.int32)[None, None, None, :] < halo_counts[..., None]
    ).astype(jnp.float32)
    lv = live[:, :, :, None, :]
    state = jnp.concatenate(
        [positions_now[:, :, :, :3, :], positions_now[:, :, :, 3:4, :] * lv, positions_next, lv], axis=3
    )
    below = shifted(state[-1:], "gx", 1)
    above = shifted(state[:1], "gx", -1)
    state = jnp.concatenate([below, state, above], axis=0)
    below = shifted(state[:, -1:], "gy", 1)
    above = shifted(state[:, :1], "gy", -1)
    state = jnp.concatenate([below, state, above], axis=1)
    if lax.axis_size("gz") == 2 and cz == 1:
        below = above = shifted(state, "gz", 1)
    else:
        below = shifted(state[:, :, -1:], "gz", 1)
        above = shifted(state[:, :, :1], "gz", -1)
    padded = jnp.concatenate([below, state, above], axis=2).reshape(-1, 8, slots)
    count = padded.shape[0]
    drift, squared = pl.pallas_call(
        functools.partial(kernel, (cx, cy, cz), width),
        out_shape=(
            jax.ShapeDtypeStruct((cells, 3, slots), jnp.float32),
            jax.ShapeDtypeStruct((cells, slots), jnp.float32),
        ),
        in_specs=[pl.BlockSpec(memory_space=pltpu.SMEM)] + [pl.BlockSpec(memory_space=pltpu.VMEM)] * 3,
        out_specs=(pl.BlockSpec(memory_space=pltpu.VMEM),) * 2,
        scratch_shapes=[
            pltpu.VMEM((count, 48, slots), jnp.bfloat16),
            pltpu.VMEM((count, 32, slots), jnp.bfloat16),
            pltpu.VMEM((count, 8, slots), jnp.float32),
        ],
    )(
        neighbour_lists.reshape(-1),
        padded,
        velocities.reshape(cells, 3, slots),
        descendants.reshape(cells, 2, slots),
    )
    total_sq, total_live = lax.psum((jnp.sum(squared), jnp.sum(live)), ("gx", "gy", "gz"))
    mean_sq = total_sq / total_live
    tension = squared / (mean_sq + 1e-06)
    return (drift.reshape(cx, cy, cz, 3, slots), tension.reshape(cx, cy, cz, slots))


def solution(mesh):
    return jax.shard_map(
        shards,
        mesh=mesh,
        in_specs=(
            P("gx", "gy", "gz", None, None),
            P("gx", "gy", "gz", None, None),
            P("gx", "gy", "gz", None, None),
            P("gx", "gy", "gz"),
            P("gx", "gy", "gz", None),
            P("gx", "gy", "gz", None, None),
        ),
        out_specs=(P("gx", "gy", "gz", None, None), P("gx", "gy", "gz", None)),
        check_vma=False,
    )
```

time: 200 us -> 115 us (0.57)
  other arithmetic: 103 us -> 5.94 us
  Pallas kernels: 0 us -> 44.8 us
  local copies, waits for them, and re-layouts: 38.2 us -> 5.09 us
  blocking collectives: 37.1 us -> 40.9 us
  waiting for transfers between devices: 10.1 us -> 6.73 us
    reduce_sum x29 -> x0, other arithmetic: 81 us -> none  [the longest x14 52.1 us: step(): return (accel + jnp.sum(diff * weight[:, None, :, :], axis=3), None)]
    pallas_call x0 -> x1, Pallas kernels: none -> 44.8 us  [shards(): pl.pallas_call(functools.partial(kernel, (cx, cy, cz), width), out_shape=...]
    gather x17 -> x0, local copies, waits for them, and re-layouts: 24.5 us -> none  [the longest x2 15.7 us: one_group(): found = jnp.transpose(next_rows[target * slots + dslot], (0, 2, 1))]
    div x15 -> x1, other arithmetic: 11.4 us -> 1.33 us  [shards(): tension = squared / (mean_sq + 1e-06)]
    transpose x2 -> x0, local copies, waits for them, and re-layouts: 6.04 us -> none  [predict(): jnp.transpose(flat[:, 4:7, :], (0, 2, 1)).reshape(px * py * pz * slots, 3)]
    psum x1, blocking collectives: 37.1 us -> 40.9 us  [shards(): lax.psum((jnp.sum(squared), jnp.sum(live)), ('gx', 'gy', 'gz'))]
    ppermute x5, waiting for transfers between devices: 10.1 us -> 6.73 us  [shifted(): lax.ppermute(shard, axis, [(i, (i + by) % peers) for i in range(peers)])]
    add x44 -> x0, other arithmetic: 2.52 us -> none  [the longest x14 1.32 us: step(): spot = offset[:, :, None] + source[:, :3, :]]
  transfers between devices with their start and end apart: 5 -> 5, of which waited for: 3 -> 4; matrix products, arithmetic and copies ran while one was open for 2% -> 3% of each run, Pallas kernels for 0% -> 0%
where the time goes in v1:
time: 115 us; the launch traced here: 114 us
  Pallas kernels  44.8 us (39%)
  blocking collectives  40.9 us (36%)
  starting transfers between devices  8.58 us (7%)
  waiting for transfers between devices  6.73 us (6%)
  other arithmetic  5.94 us (5%)
  local copies, waits for them, and re-layouts  5.09 us (4%)
  between operations  2.1 us (2%)
    pallas_call x1, Pallas kernels, shards(): pl.pallas_call(functools.partial(kernel, (cx, cy, cz), width), out_shape=...  44.8 us
    psum x1, blocking collectives, shards(): lax.psum((jnp.sum(squared), jnp.sum(live)), ('gx', 'gy', 'gz'))  40.9 us
    ppermute x5, starting transfers between devices, shifted(): lax.ppermute(shard, axis, [(i, (i + by) % peers) for i in range(peers)])  8.58 us
    ppermute x5, waiting for transfers between devices, shifted(): lax.ppermute(shard, axis, [(i, (i + by) % peers) for i in range(peers)])  6.73 us
  transfers between devices with their start and end apart: 5, of which 4 were waited for; matrix products, arithmetic and copies ran while one was open for 3% of the time, Pallas kernels for 0%

profile of v1, /device:TPU:0, one launch (start us, length us, event | category | flops | bytes accessed | tf_op | source)
XLA Modules:
  0.0 114.1 jit_solution(18193686413847689275)
XLA Ops:
  0.6 0.0 copy-start.2
  0.6 0.8 copy.25
  1.4 0.1 compare_convert_fusion
  1.5 0.8 compare_select_fusion
  2.4 0.0 copy-done.2
  2.4 0.0 copy-start
  2.4 0.8 copy-done
  3.2 3.1 %collective-permute-start = (f32[1,4,1,8,128]{4,2,3,1,0:T(1,128)S(1)}, f32[1,4,1,8,128]{4,2,3,1,0:T(1,128)S(1)}, u32[]{:S(2)}, u32[]{:S(2)}) collective-permute-start(f32[1,4,1,8,128]{4,2,3,1,0:T(1,128)S(1)} %get-tuple-element.16), channel_id=1, source_target_pairs={{0,8},{8,16},{16,24},{24,0},{1,9},{9,17},{17,25},{25,1},{2,10},{10... | collective-permute-start | bytes 49160 | tf_op jit(solution)/shard_map/ppermute | solution.py:17
  6.3 2.1 %collective-permute-start.1 = (f32[1,4,1,8,128]{4,2,3,1,0:T(1,128)S(1)}, f32[1,4,1,8,128]{4,2,3,1,0:T(1,128)S(1)}, u32[]{:S(2)}, u32[]{:S(2)}) collective-permute-start(f32[1,4,1,8,128]{4,2,3,1,0:T(1,128)S(1)} %get-tuple-element.17), channel_id=1, source_target_pairs={{0,24},{8,0},{16,8},{24,16},{1,25},{9,1},{17,9},{25,17},{2,26},{10... | collective-permute-start | bytes 49160 | tf_op jit(solution)/shard_map/ppermute | solution.py:17
  8.4 1.8 %collective-permute-done = f32[1,4,1,8,128]{4,2,3,1,0:T(1,128)S(1)} collective-permute-done((f32[1,4,1,8,128]{4,2,3,1,0:T(1,128)S(1)}, f32[1,4,1,8,128]{4,2,3,1,0:T(1,128)S(1)}, u32[]{:S(2)}, u32[]{:S(2)}) %collective-permute-start) | collective-permute-done | bytes 16416 | tf_op jit(solution)/shard_map/ppermute | solution.py:17
  10.2 0.1 collective-permute-done.1
  10.2 0.1 pad_maximum_fusion.7
  10.3 0.1 collective-permute-start.2
  10.4 0.0 copy-start.3
  10.4 1.7 %collective-permute-start.3 = (f32[10,1,1,8,128]{4,2,3,1,0:T(1,128)S(1)}, f32[10,1,1,8,128]{4,2,3,1,0:T(1,128)S(1)}, u32[]{:S(2)}, u32[]{:S(2)}) collective-permute-start(f32[10,1,1,8,128]{4,2,3,1,0:T(1,128)S(1)} %get-tuple-element.15), channel_id=1, source_target_pairs={{0,6},{2,0},{4,2},{6,4},{1,7},{3,1},{5,3},{7,5},{8,14},{10,8},{12,... | collective-permute-start | bytes 122888 | tf_op jit(solution)/shard_map/ppermute | solution.py:17
  12.1 1.7 %collective-permute-done.2 = f32[10,1,1,8,128]{4,2,3,1,0:T(1,128)S(1)} collective-permute-done((f32[10,1,1,8,128]{4,2,3,1,0:T(1,128)S(1)}, f32[10,1,1,8,128]{4,2,3,1,0:T(1,128)S(1)}, u32[]{:S(2)}, u32[]{:S(2)}) %collective-permute-start.2) | collective-permute-done | bytes 40992 | tf_op jit(solution)/shard_map/ppermute | solution.py:17
  13.8 0.0 collective-permute-done.3
  13.8 0.2 pad_maximum_fusion.1
  14.0 1.6 %collective-permute-start.4 = (f32[10,6,1,8,128]{4,2,3,1,0:T(1,128)S(1)}, f32[10,6,1,8,128]{4,2,3,1,0:T(1,128)S(1)}, u32[]{:S(2)}, u32[]{:S(2)}) collective-permute-start(f32[10,6,1,8,128]{4,2,3,1,0:T(1,128)S(1)} %pad_maximum_fusion.1), channel_id=1, source_target_pairs={{0,1},{1,0},{2,3},{3,2},{4,5},{5,4},{6,7},{7,6},{8,9},{9,8},{10,11... | collective-permute-start | bytes 737288 | tf_op jit(solution)/shard_map/ppermute | solution.py:17
  15.6 0.0 copy-done.3
  15.6 0.0 copy-start.4
  15.7 0.7 copy.29.vel
  16.3 0.5 broadcast.31
  16.8 0.0 copy-done.4
  16.8 0.7 reduce.3
  17.5 0.0 copy-start.5
  17.5 0.7 reshape.46.lists
  18.2 0.0 copy-done.5
  18.2 0.7 convert_reduce_fusion
  19.0 3.2 %collective-permute-done.4 = f32[10,6,1,8,128]{4,2,3,1,0:T(1,128)S(1)} collective-permute-done((f32[10,6,1,8,128]{4,2,3,1,0:T(1,128)S(1)}, f32[10,6,1,8,128]{4,2,3,1,0:T(1,128)S(1)}, u32[]{:S(2)}, u32[]{:S(2)}) %collective-permute-start.4) | collective-permute-done | bytes 245792 | tf_op jit(solution)/shard_map/ppermute | solution.py:17
  22.2 0.6 pad_maximum_fusion
  22.8 0.9 copy.27
  23.7 44.8 %shard_map.77 = (f32[32,3,128]{2,1,0:T(4,128)}, f32[32,128]{1,0:T(8,128)}) custom-call(s32[448]{0:T(512)} %reshape.46.lists, f32[180,8,128]{2,1,0:T(8,128)} %bitcast.9, f32[32,3,128]{2,1,0:T(4,128)} %copy.29.vel, s32[32,2,128]{2,1,0:T(2,128)} %bitcast.14), custom_call_target="tpu_custom_call" | custom-call | tf_op jit(solution)/shard_map/pallas_call | solution.py:127
  68.5 0.0 copy-start.1
  68.5 1.4 %reduce_sum.18 = f32[]{:T(128)} reduce(f32[32,128]{1,0:T(8,128)} %get-tuple-element.5, f32[]{:T(128)} %constant.1.clone.1), dimensions={0,1}, to_apply=%region_0.0 | reduce | flops 4095 | bytes 16392 | tf_op jit(solution)/shard_map/reduce_sum | solution.py:146
  69.9 40.9 %all-reduce = (f32[]{:T(128)}, f32[]{:T(128)}) all-reduce(f32[]{:T(128)} %reduce_sum.18, f32[]{:T(128)} %convert_reduce_fusion), channel_id=1, replica_groups=mesh['gx'=4,'gy'=4,'gz'=2] {'gx','gy','gz'}, use_global_device_ids=true, to_apply=%region_1.0 | all-reduce | flops 2 | bytes 16 | tf_op jit(solution)/shard_map/psum | solution.py:146
  112.1 1.3 %broadcast_divide_fusion = f32[32,128]{1,0:T(8,128)} fusion(f32[32,128]{1,0:T(8,128)} %get-tuple-element.5, f32[]{:T(128)S(6)} %add.7), kind=kLoop, calls=%fused_computation.16 | loop fusion | flops 4096 | bytes 32772 | tf_op jit(solution)/shard_map/div | solution.py:148
  113.4 0.0 copy-done.1
  113.4 0.7 copy.30
  (3 shorter events, 0.1 us)
Async XLA Ops:
  0.6 1.7 %copy-start.2 = (f32[8,4,1,4,128]{4,3,2,1,0:T(4,128)S(1)}, f32[8,4,1,4,128]{4,3,2,1,0:T(4,128)}, u32[]{:S(2)}) copy-start(f32[8,4,1,4,128]{4,3,2,1,0:T(4,128)} %param.6) | copy-start | bytes 196612
  2.4 0.8 copy-start
  3.2 6.9 %collective-permute-start = (f32[1,4,1,8,128]{4,2,3,1,0:T(1,128)S(1)}, f32[1,4,1,8,128]{4,2,3,1,0:T(1,128)S(1)}, u32[]{:S(2)}, u32[]{:S(2)}) collective-permute-start(f32[1,4,1,8,128]{4,2,3,1,0:T(1,128)S(1)} %get-tuple-element.16), channel_id=1, source_target_pairs={{0,8},{8,16},{16,24},{24,0},{1,9},{9,17},{17,25},{25,1},{2,10},{10... | collective-permute-start | bytes 49160 | tf_op jit(solution)/shard_map/ppermute | solution.py:17
  6.3 3.9 %collective-permute-start.1 = (f32[1,4,1,8,128]{4,2,3,1,0:T(1,128)S(1)}, f32[1,4,1,8,128]{4,2,3,1,0:T(1,128)S(1)}, u32[]{:S(2)}, u32[]{:S(2)}) collective-permute-start(f32[1,4,1,8,128]{4,2,3,1,0:T(1,128)S(1)} %get-tuple-element.17), channel_id=1, source_target_pairs={{0,24},{8,0},{16,8},{24,16},{1,25},{9,1},{17,9},{25,17},{2,26},{10... | collective-permute-start | bytes 49160 | tf_op jit(solution)/shard_map/ppermute | solution.py:17
  10.3 3.5 %collective-permute-start.2 = (f32[10,1,1,8,128]{4,2,3,1,0:T(1,128)S(1)}, f32[10,1,1,8,128]{4,2,3,1,0:T(1,128)S(1)}, u32[]{:S(2)}, u32[]{:S(2)}) collective-permute-start(f32[10,1,1,8,128]{4,2,3,1,0:T(1,128)S(1)} %get-tuple-element.14), channel_id=1, source_target_pairs={{0,2},{2,4},{4,6},{6,0},{1,3},{3,5},{5,7},{7,1},{8,10},{10,12},{12... | collective-permute-start | bytes 122888 | tf_op jit(solution)/shard_map/ppermute | solution.py:17
  10.4 5.3 %copy-start.3 = (f32[8,4,1,3,128]{4,2,3,1,0:T(1,128)S(1)}, f32[8,4,1,3,128]{4,2,3,1,0:T(1,128)}, u32[]{:S(2)}) copy-start(f32[8,4,1,3,128]{4,2,3,1,0:T(1,128)} %param.7) | copy-start | bytes 147460
  10.4 3.4 %collective-permute-start.3 = (f32[10,1,1,8,128]{4,2,3,1,0:T(1,128)S(1)}, f32[10,1,1,8,128]{4,2,3,1,0:T(1,128)S(1)}, u32[]{:S(2)}, u32[]{:S(2)}) collective-permute-start(f32[10,1,1,8,128]{4,2,3,1,0:T(1,128)S(1)} %get-tuple-element.15), channel_id=1, source_target_pairs={{0,6},{2,0},{4,2},{6,4},{1,7},{3,1},{5,3},{7,5},{8,14},{10,8},{12,... | collective-permute-start | bytes 122888 | tf_op jit(solution)/shard_map/ppermute | solution.py:17
  14.0 8.2 %collective-permute-start.4 = (f32[10,6,1,8,128]{4,2,3,1,0:T(1,128)S(1)}, f32[10,6,1,8,128]{4,2,3,1,0:T(1,128)S(1)}, u32[]{:S(2)}, u32[]{:S(2)}) collective-permute-start(f32[10,6,1,8,128]{4,2,3,1,0:T(1,128)S(1)} %pad_maximum_fusion.1), channel_id=1, source_target_pairs={{0,1},{1,0},{2,3},{3,2},{4,5},{5,4},{6,7},{7,6},{8,9},{9,8},{10,11... | collective-permute-start | bytes 737288 | tf_op jit(solution)/shard_map/ppermute | solution.py:17
  15.6 1.2 %copy-start.4 = (s32[8,4,1,14]{3,2,1,0:T(1,128)S(1)}, s32[8,4,1,14]{3,2,1,0:T(1,128)}, u32[]{:S(2)}) copy-start(s32[8,4,1,14]{3,2,1,0:T(1,128)} %param.10) | copy-start | bytes 5380
  17.5 0.7 copy-start.5
  68.5 44.9 %copy-start.1 = (f32[32,3,128]{2,1,0:T(4,128)S(1)}, f32[32,3,128]{2,1,0:T(4,128)}, u32[]{:S(2)}) copy-start(f32[32,3,128]{2,1,0:T(4,128)} %get-tuple-element.4) | copy-start | bytes 147460
